TPU v7x, 32 devices: a whole 2x2x4 slice. The times are simulated.
32 devices in a mesh: groups: 2 (over x), freq: 16 (over z, y, core).
Axes of the slice: x: 2, y: 2, z: 4, core: 2. Of those that a mesh axis runs over, the one named last changes fastest.
Arguments:
- traces: bfloat16 [1024, 2048, 32], P('freq', None, 'groups'), parts along dimension 2, may hold values from -6 to 6
- freq_index: int32 [16], replicated, may hold values from 1 to 511
- block_map: int32 [64, 64], replicated, may hold values 0 or 1
- green_rec: bfloat16 [16, 2, 2048, 1536], P('freq', None, None, 'groups'), parts along dimension 3, may hold values from -0.1875 to 0.1875
- green_src: bfloat16 [16, 2, 16, 1536], P('freq', None, None, 'groups'), parts along dimension 3, may hold values from -0.25 to 0.25
Outputs:
- image: float32 [1536], P(('groups', 'freq')), parts along dimension 0
There are 2 independent parts, one for each index of `groups`. A program takes and returns all parts, laid end to end along the dimension named above; an argument that names none is the same for every part. Nothing has to cross between parts.
Inputs may be any that keep to these rules, and one draw needn't show every extreme that they name: `freq_index`: frequency bins; they may repeat. `block_map`: 1 where a receiver block lies in an image tile's aperture.
All inputs are finite; a program needn't handle non-finite values.
Results may differ from a plain program's by a relative error of at most 0.0038.
Values may be sent and summed in bfloat16 or wider, within the bound.
No kernel may reach another device: no remote copies, remote signals or barrier semaphores. Data moves between devices by JAX's collectives and lax.ppermute only.
A program may use at most 64 MiB of HBM per device.

v0:
```python
import math
import jax
import jax.numpy as jnp
from jax import lax
from jax.sharding import PartitionSpec as P


def dft_table(freq_index, length):
    sample_index = jnp.arange(length, dtype=jnp.int32)
    phases = freq_index[:, None] * sample_index[None, :] % length
    angles = phases.astype(jnp.float32) * jnp.float32(2.0 * math.pi / length)
    stacked = jnp.stack((jnp.cos(angles), -jnp.sin(angles)), axis=1)
    return stacked.reshape(freq_index.shape[0] * 2, length).astype(jnp.bfloat16)


def expand_map(block_map, receivers, points):
    row_span = receivers // block_map.shape[0]
    col_span = points // block_map.shape[1]
    return jnp.repeat(jnp.repeat(block_map, row_span, axis=0), col_span, axis=1).astype(
        jnp.bfloat16
    )


def transform(cos_table, records, length):
    spectrum = jnp.dot(cos_table, records.reshape(length, -1), preferred_element_type=jnp.float32)
    return (spectrum * (1.0 / math.sqrt(length))).astype(jnp.bfloat16)


def back_project(spectra, masked):
    swapped = jnp.stack((spectra[:, 1], -spectra[:, 0]), axis=1)
    blocks = jnp.stack((spectra, swapped), axis=1)
    return jnp.einsum("fcrx,focrs->fosx", masked, blocks, preferred_element_type=jnp.float32)


def body(traces, freq_index, block_map, green_rec, green_src):
    shards = lax.axis_size("freq")
    length = traces.shape[0] * shards
    receivers = traces.shape[1]
    shots = traces.shape[2]
    freqs = freq_index.shape[0]
    cos_table = dft_table(freq_index, length)
    masked = green_rec * expand_map(block_map, receivers, green_rec.shape[3])[None, None]
    regrouped = lax.all_to_all(traces, "freq", split_axis=2, concat_axis=0, tiled=True)
    spectrum = transform(cos_table, regrouped, length).reshape(freqs, 2, receivers, shots // shards)
    gathered = lax.all_to_all(spectrum, "freq", split_axis=0, concat_axis=3, tiled=True)
    back_field = back_project(gathered, masked)
    partial_image = jnp.sum(green_src.astype(jnp.float32) * back_field, axis=(0, 1, 2))
    return lax.psum_scatter(partial_image, "freq", scatter_dimension=0, tiled=True)


def solution(mesh):
    in_specs = (
        P("freq", None, "groups"),
        P(),
        P(),
        P("freq", None, None, "groups"),
        P("freq", None, None, "groups"),
    )
    out_specs = P(("groups", "freq"))
    return jax.shard_map(body, mesh=mesh, in_specs=in_specs, out_specs=out_specs, check_vma=False)
```

profile of v0, /device:TPU:0, one launch (start us, length us, event | category | flops | bytes accessed | tf_op | source)
XLA Modules:
  0.0 166.9 jit_solution(11297971137079490773)
XLA Ops:
  0.0 6.4 %copy.26 = bf16[64,2048,16]{1,0,2:T(8,128)(2,1)} copy(bf16[64,2048,16]{1,2,0:T(8,128)(2,1)} %param.5) | data formatting | bytes 8388608 | tf_op args[0]
  6.4 0.0 copy-start.2
  6.5 7.6 %all-to-all-start = ((bf16[64,2048,16]{1,0,2:T(8,128)(2,1)}), bf16[64,2048,16]{1,0,2:T(8,128)(2,1)}, u32[]{:S(2)}, u32[]{:S(2)}) async-start(bf16[64,2048,16]{1,0,2:T(8,128)(2,1)} %copy.26), calls=%async_computation | async-start | bytes 8388608 | tf_op jit(solution)/shard_map/all_to_all | solution.py:43
  14.1 0.0 copy-done.2
  14.1 0.0 copy-start.1
  14.1 0.3 cosine_convert_fusion
  14.4 0.1 copy.25
  14.6 77.0 %all-to-all-done = bf16[64,2048,16]{1,0,2:T(8,128)(2,1)} async-done(((bf16[64,2048,16]{1,0,2:T(8,128)(2,1)}), bf16[64,2048,16]{1,0,2:T(8,128)(2,1)}, u32[]{:S(2)}, u32[]{:S(2)}) %all-to-all-start) | async-done | bytes 4194336 | tf_op jit(solution)/shard_map/all_to_all | solution.py:43
  91.6 3.0 %fusion.4 = bf16[32,2048]{1,0:T(8,128)(2,1)S(1)} fusion(bf16[32,1024]{1,0:T(8,128)(2,1)S(1)} %convert_element_type.47, bf16[1024,2048]{1,0:T(8,128)(2,1)} %bitcast.2), kind=kOutput, calls=%fused_computation.5 | convolution fusion | flops 134348800 | bytes 4390912 | tf_op jit(solution)/shard_map/dot_general | solution.py:25
  94.6 0.8 reshape.132
  95.4 19.6 %all-to-all-start.1 = ((bf16[16,2,2048,1]{2,1,3,0:T(2,128)(2,1)}), bf16[16,2,2048,1]{2,1,3,0:T(2,128)(2,1)S(1)}, u32[]{:S(2)}, u32[]{:S(2)}) async-start(bf16[16,2,2048,1]{2,1,3,0:T(2,128)(2,1)} %bitcast.3), calls=%async_computation.1 | async-start | bytes 262144 | tf_op jit(solution)/shard_map/all_to_all | solution.py:45
  115.0 0.0 copy-done.1
  115.1 0.1 broadcast_in_dim.4
  115.1 0.2 copy.29
  115.3 2.5 %broadcast_in_dim.10 = bf16[2048,64,12]{0,2,1:T(8,128)(2,1)} broadcast(bf16[2048,64]{0,1:T(8,128)(2,1)S(1)} %copy.29), dimensions={0,1} | broadcast | bytes 3407872 | tf_op jit(solution)/shard_map/broadcast_in_dim | solution.py:19
  117.8 6.2 %convert_element_type.51 = bf16[2048,768]{0,1:T(8,128)(2,1)} reshape(bf16[2048,64,12]{0,2,1:T(8,128)(2,1)} %broadcast_in_dim.10) | data formatting | bytes 6291456 | tf_op jit(solution)/shard_map/convert_element_type | solution.py:19
  124.0 0.0 copy-start.3
  124.0 0.0 copy-start
  124.0 3.2 %copy.30 = bf16[2048,768]{1,0:T(8,128)(2,1)S(1)} copy(bf16[2048,768]{0,1:T(8,128)(2,1)} %convert_element_type.51) | data formatting | bytes 6291456 | tf_op jit(solution)/shard_map/convert_element_type | solution.py:19
  127.2 0.0 copy-done.3
  127.2 0.6 dynamic-slice
  128.4 0.0 all-to-all-done.1
  128.5 0.0 copy-done
  128.5 4.0 %fusion.11 = f32[768]{0:T(1024)S(1)} fusion(bf16[1,2,2048,768]{3,2,1,0:T(8,128)(2,1)} %param.8, bf16[2048,768]{1,0:T(8,128)(2,1)S(1)} %copy.30, bf16[1,1,2,2048,16]{3,4,2,1,0:T(8,128)(2,1)S(1)} %maximum_bitcast_fusion.2, bf16[1,1,2,2048,16]{3,4,2,1,0:T(8,128)(2,1)S(1)} %bitcast.47, bf16[1,2,16,768]{3,2,1,0:T(8,128)(2,1)S(1)} %copy-done), kind=kOutput, calls=%fused_computation.8 | convolution fusion | flops 204676352 | bytes 9751552 | tf_op jit(solution)/shard_map/fcrx,focrs->fosx/dot_general | solution.py:32
  132.5 33.8 %all-reduce = f32[768]{0:T(1024)S(1)} all-reduce(f32[768]{0:T(1024)S(1)} %fusion.11), channel_id=2, replica_groups=mesh['groups'=2,'freq'=16] {'freq'}, use_global_device_ids=true, to_apply=%region_1.2.clone | all-reduce | flops 768 | bytes 6144
  166.3 0.6 dynamic-slice.1
  (6 shorter events, 0.1 us)
Async XLA Ops:
  6.4 7.6 %copy-start.2 = (s32[16]{0:T(128)S(1)}, s32[16]{0:T(128)}, u32[]{:S(2)}) copy-start(s32[16]{0:T(128)} %param.6) | copy-start | bytes 196
  6.5 85.1 %all-to-all-start = ((bf16[64,2048,16]{1,0,2:T(8,128)(2,1)}), bf16[64,2048,16]{1,0,2:T(8,128)(2,1)}, u32[]{:S(2)}, u32[]{:S(2)}) async-start(bf16[64,2048,16]{1,0,2:T(8,128)(2,1)} %copy.26), calls=%async_computation | async-start | bytes 8388608 | tf_op jit(solution)/shard_map/all_to_all | solution.py:43
  14.1 101.0 %copy-start.1 = (s32[64,64]{1,0:T(8,128)S(1)}, s32[64,64]{1,0:T(8,128)}, u32[]{:S(2)}) copy-start(s32[64,64]{1,0:T(8,128)} %param.7) | copy-start | bytes 49156
  95.4 33.1 %all-to-all-start.1 = ((bf16[16,2,2048,1]{2,1,3,0:T(2,128)(2,1)}), bf16[16,2,2048,1]{2,1,3,0:T(2,128)(2,1)S(1)}, u32[]{:S(2)}, u32[]{:S(2)}) async-start(bf16[16,2,2048,1]{2,1,3,0:T(2,128)(2,1)} %bitcast.3), calls=%async_computation.1 | async-start | bytes 262144 | tf_op jit(solution)/shard_map/all_to_all | solution.py:45
  124.0 3.2 %copy-start.3 = (u32[32]{0:T(128)S(1)}, u32[32]{0:T(128)}, u32[]{:S(2)}) copy-start(u32[32]{0:T(128)} %constant.25) | copy-start | bytes 388
  124.0 4.6 %copy-start = (bf16[1,2,16,768]{3,2,1,0:T(8,128)(2,1)S(1)}, bf16[1,2,16,768]{3,2,1,0:T(8,128)(2,1)}, u32[]{:S(2)}) copy-start(bf16[1,2,16,768]{3,2,1,0:T(8,128)(2,1)} %param.9) | copy-start | bytes 147460
where the time goes:
time: 168 us; the launch traced here: 167 us
  waiting for transfers between devices  77.1 us (46%)
  blocking collectives  33.8 us (20%)
  starting transfers between devices  27.2 us (16%)
  local copies, waits for them, and re-layouts  20.6 us (12%)
  matrix products  6.97 us (4%)
    all_to_all x1, waiting for transfers between devices, body(): lax.all_to_all(traces, 'freq', split_axis=2, concat_axis=0, tiled=True)  77 us
    unnamed x1, blocking collectives  33.8 us
    all_to_all x1, starting transfers between devices, body(): lax.all_to_all(spectrum, 'freq', split_axis=0, concat_axis=3, tiled=True)  19.6 us
    convert_element_type x3, local copies, waits for them, and re-layouts, expand_map(): jnp.repeat(jnp.repeat(block_map, row_span, axis=0), col_span, axis=1)  9.56 us
    unnamed x11, local copies, waits for them, and re-layouts  7.64 us
    all_to_all x1, starting transfers between devices, body(): lax.all_to_all(traces, 'freq', split_axis=2, concat_axis=0, tiled=True)  7.6 us
    dot_general x1, matrix products, back_project(): jnp.einsum('fcrx,focrs->fosx', masked, blocks, preferred_element_type=jnp...  3.96 us
  transfers between devices with their start and end apart: 2, of which 1 were waited for; matrix products, arithmetic and copies ran while one was open for 8% of the time, Pallas kernels for 0%

commit v1 on v0

--- a/solution.py
+++ b/solution.py
@@ -3,6 +3,13 @@
 import jax.numpy as jnp
 from jax import lax
 from jax.sharding import PartitionSpec as P
+
+
+def form_digits(incoming_x):
+    far_arr = lax.axis_size("freq")
+    t1 = jnp.split(incoming_x, far_arr, axis=2)
+    tmp = lax.all_to_all(jnp.stack(t1, axis=0), "freq", 0, 0)
+    return jnp.concatenate(tmp, axis=0)
 
 
 def dft_table(freq_index, length):
@@ -40,7 +47,7 @@
     freqs = freq_index.shape[0]
     cos_table = dft_table(freq_index, length)
     masked = green_rec * expand_map(block_map, receivers, green_rec.shape[3])[None, None]
-    regrouped = lax.all_to_all(traces, "freq", split_axis=2, concat_axis=0, tiled=True)
+    regrouped = form_digits(traces)
     spectrum = transform(cos_table, regrouped, length).reshape(freqs, 2, receivers, shots // shards)
     gathered = lax.all_to_all(spectrum, "freq", split_axis=0, concat_axis=3, tiled=True)
     back_field = back_project(gathered, masked)

time: 168 us -> 192 us (1.14)
  local copies, waits for them, and re-layouts: 20.6 us -> 45.4 us
    split x0 -> x1, local copies, waits for them, and re-layouts: none -> 17.6 us  [form_digits(): t1 = jnp.split(incoming_x, far_arr, axis=2)]
    unnamed x11 -> x25, local copies, waits for them, and re-layouts: 7.64 us -> 14 us
  transfers between devices with their start and end apart: 2 -> 2, of which waited for: 1 -> 1; matrix products, arithmetic and copies ran while one was open for 8% -> 7% of each run, Pallas kernels for 0% -> 0%
where the time goes in v1:
time: 192 us
  waiting for transfers between devices  77 us (40%)
  local copies, waits for them, and re-layouts  45.4 us (24%)
  blocking collectives  33.8 us (18%)
  starting transfers between devices  27.2 us (14%)
  matrix products  6.97 us (4%)
    all_to_all x1, waiting for transfers between devices, form_digits(): tmp = lax.all_to_all(jnp.stack(t1, axis=0), 'freq', 0, 0)  77 us
    unnamed x1, blocking collectives  33.8 us
    all_to_all x1, starting transfers between devices, body(): lax.all_to_all(spectrum, 'freq', split_axis=0, concat_axis=3, tiled=True)  19.6 us
    split x1, local copies, waits for them, and re-layouts, form_digits(): t1 = jnp.split(incoming_x, far_arr, axis=2)  17.6 us
    unnamed x25, local copies, waits for them, and re-layouts  14 us
    convert_element_type x3, local copies, waits for them, and re-layouts, expand_map(): jnp.repeat(jnp.repeat(block_map, row_span, axis=0), col_span, axis=1)  9.55 us
    all_to_all x1, starting transfers between devices, form_digits(): tmp = lax.all_to_all(jnp.stack(t1, axis=0), 'freq', 0, 0)  7.6 us
    dot_general x1, matrix products, back_project(): jnp.einsum('fcrx,focrs->fosx', masked, blocks, preferred_element_type=jnp...  3.96 us
  transfers between devices with their start and end apart: 2, of which 1 were waited for; matrix products, arithmetic and copies ran while one was open for 7% of the time, Pallas kernels for 0%

profile of v1, /device:TPU:0, one launch (start us, length us, event | category | flops | bytes accessed | tf_op | source)
XLA Modules:
  0.0 191.7 jit_solution(3591067616009023110)
XLA Ops:
  0.0 17.6 %fusion.39 = (bf16[64,2048,1]{1,2,0:T(2,128)(2,1)S(1)}, bf16[64,2048,1]{1,2,0:T(2,128)(2,1)S(1)}, bf16[64,2048,1]{1,2,0:T(2,128)(2,1)S(1)}, bf16[64,2048,1]{1,2,...) fusion(bf16[64,2048,16]{1,2,0:T(8,128)(2,1)} %param.5), kind=kLoop, calls=%fused_computation.61 | loop fusion | bytes 8388608 | tf_op jit(solution)/shard_map/split | solution.py:10
  17.6 0.8 fusion.31
  18.4 0.9 fusion.30
  19.3 0.9 fusion.29
  20.1 0.9 fusion.28
  21.0 0.8 fusion.27
  21.9 0.9 fusion.26
  22.7 0.9 fusion.25
  23.6 0.8 fusion.24
  24.4 0.8 fusion.23
  25.3 0.9 fusion.22
  26.1 0.9 fusion.21
  27.0 0.9 fusion.20
  27.8 0.9 fusion.19
  28.7 0.8 fusion.18
  29.5 0.9 fusion.17
  30.4 0.9 fusion.16
  31.3 7.6 %all-to-all-start = ((bf16[16,64,2048,1]{2,1,3,0:T(8,128)(2,1)}), bf16[16,64,2048,1]{2,1,3,0:T(8,128)(2,1)}, u32[]{:S(2)}, u32[]{:S(2)}) async-start(bf16[16,64,2048,1]{2,1,3,0:T(8,128)(2,1)} %fusion.16), calls=%async_computation | async-start | bytes 8388608 | tf_op jit(solution)/shard_map/all_to_all | solution.py:11
  38.9 0.3 cosine_convert_fusion
  39.4 77.0 %all-to-all-done = bf16[16,64,2048,1]{2,1,3,0:T(8,128)(2,1)} async-done(((bf16[16,64,2048,1]{2,1,3,0:T(8,128)(2,1)}), bf16[16,64,2048,1]{2,1,3,0:T(8,128)(2,1)}, u32[]{:S(2)}, u32[]{:S(2)}) %all-to-all-start) | async-done | bytes 4194336 | tf_op jit(solution)/shard_map/all_to_all | solution.py:11
  116.4 3.0 %fusion.4 = bf16[32,2048]{1,0:T(8,128)(2,1)S(1)} fusion(bf16[32,1024]{1,0:T(8,128)(2,1)S(1)} %convert_element_type.47, bf16[1024,2048]{1,0:T(8,128)(2,1)} %bitcast.16), kind=kOutput, calls=%fused_computation.5 | convolution fusion | flops 134348800 | bytes 4390912 | tf_op jit(solution)/shard_map/dot_general | solution.py:32
  119.5 0.7 reshape.127
  120.2 19.6 %all-to-all-start.1 = ((bf16[16,2,2048,1]{2,1,3,0:T(2,128)(2,1)}), bf16[16,2,2048,1]{2,1,3,0:T(2,128)(2,1)S(1)}, u32[]{:S(2)}, u32[]{:S(2)}) async-start(bf16[16,2,2048,1]{2,1,3,0:T(2,128)(2,1)} %bitcast.17), calls=%async_computation.1 | async-start | bytes 262144 | tf_op jit(solution)/shard_map/all_to_all | solution.py:52
  139.9 0.1 broadcast_in_dim.4
  140.0 0.2 copy.119
  140.2 2.5 %broadcast_in_dim.10 = bf16[2048,64,12]{0,2,1:T(8,128)(2,1)} broadcast(bf16[2048,64]{0,1:T(8,128)(2,1)S(1)} %copy.119), dimensions={0,1} | broadcast | bytes 3407872 | tf_op jit(solution)/shard_map/broadcast_in_dim | solution.py:26
  142.6 6.2 %convert_element_type.51 = bf16[2048,768]{0,1:T(8,128)(2,1)} reshape(bf16[2048,64,12]{0,2,1:T(8,128)(2,1)} %broadcast_in_dim.10) | data formatting | bytes 6291456 | tf_op jit(solution)/shard_map/convert_element_type | solution.py:26
  148.8 3.2 %copy.120 = bf16[2048,768]{1,0:T(8,128)(2,1)S(1)} copy(bf16[2048,768]{0,1:T(8,128)(2,1)} %convert_element_type.51) | data formatting | bytes 6291456 | tf_op jit(solution)/shard_map/convert_element_type | solution.py:26
  152.0 0.6 dynamic-slice
  153.4 4.0 %fusion.11 = f32[768]{0:T(1024)S(1)} fusion(bf16[1,2,2048,768]{3,2,1,0:T(8,128)(2,1)} %param.8, bf16[2048,768]{1,0:T(8,128)(2,1)S(1)} %copy.120, bf16[1,1,2,2048,16]{3,4,2,1,0:T(8,128)(2,1)S(1)} %maximum_bitcast_fusion.2, bf16[1,1,2,2048,16]{3,4,2,1,0:T(8,128)(2,1)S(1)} %bitcast.107, bf16[1,2,16,768]{3,2,1,0:T(8,128)(2,1)S(1)} %copy-done), kind=kOutput, calls=%fused_computation.8 | convolution fusion | flops 204676352 | bytes 9751552 | tf_op jit(solution)/shard_map/fcrx,focrs->fosx/dot_general | solution.py:39
  157.3 33.8 %all-reduce = f32[768]{0:T(1024)S(1)} all-reduce(f32[768]{0:T(1024)S(1)} %fusion.11), channel_id=2, replica_groups=mesh['groups'=2,'freq'=16] {'freq'}, use_global_device_ids=true, to_apply=%region_1.2.clone | all-reduce | flops 768 | bytes 6144
  191.2 0.6 dynamic-slice.1
  (16 shorter events, 0.2 us)
Async XLA Ops:
  31.3 7.6 %copy-start.2 = (s32[16]{0:T(128)S(1)}, s32[16]{0:T(128)}, u32[]{:S(2)}) copy-start(s32[16]{0:T(128)} %param.6) | copy-start | bytes 196
  31.3 85.1 %all-to-all-start = ((bf16[16,64,2048,1]{2,1,3,0:T(8,128)(2,1)}), bf16[16,64,2048,1]{2,1,3,0:T(8,128)(2,1)}, u32[]{:S(2)}, u32[]{:S(2)}) async-start(bf16[16,64,2048,1]{2,1,3,0:T(8,128)(2,1)} %fusion.16), calls=%async_computation | async-start | bytes 8388608 | tf_op jit(solution)/shard_map/all_to_all | solution.py:11
  38.9 101.0 %copy-start.1 = (s32[64,64]{1,0:T(8,128)S(1)}, s32[64,64]{1,0:T(8,128)}, u32[]{:S(2)}) copy-start(s32[64,64]{1,0:T(8,128)} %param.7) | copy-start | bytes 49156
  120.2 33.0 %all-to-all-start.1 = ((bf16[16,2,2048,1]{2,1,3,0:T(2,128)(2,1)}), bf16[16,2,2048,1]{2,1,3,0:T(2,128)(2,1)S(1)}, u32[]{:S(2)}, u32[]{:S(2)}) async-start(bf16[16,2,2048,1]{2,1,3,0:T(2,128)(2,1)} %bitcast.17), calls=%async_computation.1 | async-start | bytes 262144 | tf_op jit(solution)/shard_map/all_to_all | solution.py:52
  148.8 3.2 %copy-start.3 = (u32[32]{0:T(128)S(1)}, u32[32]{0:T(128)}, u32[]{:S(2)}) copy-start(u32[32]{0:T(128)} %constant.25) | copy-start | bytes 388
  148.8 4.6 %copy-start = (bf16[1,2,16,768]{3,2,1,0:T(8,128)(2,1)S(1)}, bf16[1,2,16,768]{3,2,1,0:T(8,128)(2,1)}, u32[]{:S(2)}) copy-start(bf16[1,2,16,768]{3,2,1,0:T(8,128)(2,1)} %param.9) | copy-start | bytes 147460
